TPU v7x, 256 devices: a whole 4x4x8 slice. The times are simulated.
256 devices in a mesh: row: 8 (over x, y_lo), col: 32 (over y_hi, z, core).
Axes of the slice: x: 4, y: 4 (y_hi: 2, y_lo: 2; y = y_hi * 2 + y_lo), z: 8, core: 2. Of those that a mesh axis runs over, the one named last changes fastest.
Arguments:
- mlp_param: float32 [6144, 24576], P('row', 'col'), may hold values from -250 to 250
- mlp_grad: bfloat16 [6144, 24576], P('row', 'col'), may hold values from -250 to 250
- mlp_row_state: float32 [6144], P('row'), may hold values from 0.03 to 2.7
- mlp_col_state: float32 [24576], P('col'), may hold values from 0.02 to 0.3
- attn_param: float32 [6144, 6144], P('row', 'col'), may hold values from -250 to 250
- attn_grad: bfloat16 [6144, 6144], P('row', 'col'), may hold values from -250 to 250
- attn_row_state: float32 [6144], P('row'), may hold values from 0.03 to 2.7
- attn_col_state: float32 [6144], P('col'), may hold values from 0.02 to 0.3
Outputs:
- mlp_param_new: float32 [6144, 24576], P('row', 'col')
- attn_param_new: float32 [6144, 6144], P('row', 'col')
- mlp_row_new: float32 [6144], P('row')
- mlp_col_new: float32 [24576], P('col')
- attn_row_new: float32 [6144], P('row')
- attn_col_new: float32 [6144], P('col')
- attn_copy: bfloat16 [6144, 6144], P(None, 'col')
All inputs are finite; a program needn't handle non-finite values.
Results may differ from a plain program's by a relative error of at most 0.0004.
Values may be sent and summed in bfloat16 or wider, within the bound.
No kernel may reach another device: no remote copies, remote signals or barrier semaphores. Data moves between devices by JAX's collectives and lax.ppermute only.
A program may use at most 64 MiB of HBM per device.

v0:
```python
import jax
import jax.numpy as jnp
from jax import lax
from jax.sharding import Mesh
from jax.sharding import PartitionSpec as P

STEP = 4
ROW = ("row_0", "row_1")
COL = ("col_0", "col_1", "col_2")
ROW_COL = ("row_0", "row_1", "col_0", "col_1", "col_2")
TINY_SQUARE = 1e-30
LEARN_RATE = 0.05
DECAY_POWER = 0.8


def over_axes(value, axes):
    for axis in axes:
        value = lax.psum(value, axis)
    return value


def from_everyone(value, axis):
    length = lax.axis_size(axis)
    return lax.all_to_all(
        jnp.broadcast_to(value[None], (length, *value.shape)), axis, 0, 0, tiled=True
    )


def of_everyone(value, axis):
    return from_everyone(value, axis).sum(axis=0)


def packed_total(arrays, axis):
    ends = [0]
    for a in arrays:
        ends.append(ends[-1] + a.size)
    running = of_everyone(jnp.concatenate([a.ravel() for a in arrays]), axis)
    return tuple((running[b:e].reshape(a.shape) for a, b, e in zip(arrays, ends, ends[1:])))


def in_order(pieces, dim):
    pieces = jnp.moveaxis(pieces, 0, dim)
    dims = pieces.shape
    return pieces.reshape(*dims[:dim], dims[dim] * dims[dim + 1], *dims[dim + 2 :])


def gather_directly(value, axis, dim):
    pieces = from_everyone(value, axis)
    return in_order(pieces, dim)


def local(
    mlp_param,
    mlp_grad,
    mlp_row_state,
    mlp_col_state,
    attn_param,
    attn_grad,
    attn_row_state,
    attn_col_state,
):
    keep_rate = 1.0 - STEP ** (-DECAY_POWER)
    block_rows = mlp_grad.shape[0]
    rows_total = block_rows * lax.axis_size(ROW)
    mlp_width = mlp_grad.shape[1] * lax.axis_size(COL)
    attn_width = attn_grad.shape[1] * lax.axis_size(COL)
    mlp_count = float(rows_total * mlp_width)
    attn_count = float(rows_total * attn_width)
    mlp_square = jnp.square(mlp_grad.astype(jnp.float32)) + TINY_SQUARE
    attn_square = jnp.square(attn_grad.astype(jnp.float32)) + TINY_SQUARE
    param_local = (jnp.sum(jnp.square(mlp_param)), jnp.sum(jnp.square(attn_param)))
    param_mlp, param_attn = (over_axes(param_local[0], ROW_COL), over_axes(param_local[1], ROW_COL))
    row_mlp, row_attn = packed_total(
        (jnp.sum(mlp_square, axis=1), jnp.sum(attn_square, axis=1)), COL
    )
    mlp_rows_new = keep_rate * mlp_row_state + (1.0 - keep_rate) * (row_mlp / mlp_width)
    attn_rows_new = keep_rate * attn_row_state + (1.0 - keep_rate) * (row_attn / attn_width)
    col_mlp, col_attn = packed_total(
        (jnp.sum(mlp_square, axis=0), jnp.sum(attn_square, axis=0)), ROW
    )
    mlp_cols_new = keep_rate * mlp_col_state + (1.0 - keep_rate) * (col_mlp / rows_total)
    attn_cols_new = keep_rate * attn_col_state + (1.0 - keep_rate) * (col_attn / rows_total)
    mlp_raw = mlp_grad.astype(jnp.float32) / jnp.sqrt(mlp_rows_new[:, None] * mlp_cols_new[None, :])
    attn_raw = attn_grad.astype(jnp.float32) / jnp.sqrt(
        attn_rows_new[:, None] * attn_cols_new[None, :]
    )
    clip_local = (jnp.sum(jnp.square(mlp_raw)), jnp.sum(jnp.square(attn_raw)))
    clip_mlp, clip_attn = (over_axes(clip_local[0], ROW_COL), over_axes(clip_local[1], ROW_COL))
    mlp_clip = jnp.maximum(1.0, jnp.sqrt(clip_mlp / mlp_count))
    attn_clip = jnp.maximum(1.0, jnp.sqrt(clip_attn / attn_count))
    mlp_step = LEARN_RATE * jnp.sqrt(param_mlp / mlp_count)
    attn_step = LEARN_RATE * jnp.sqrt(param_attn / attn_count)
    mlp_new = mlp_param - mlp_step * (mlp_raw / mlp_clip)
    attn_new = attn_param - attn_step * (attn_raw / attn_clip)
    weight_copy = gather_directly(attn_new.astype(jnp.bfloat16), ROW, 0)
    return (
        mlp_new,
        attn_new,
        mlp_rows_new,
        mlp_cols_new,
        attn_rows_new,
        attn_cols_new,
        weight_copy,
    )


def solution(mesh):
    finer = Mesh(mesh.devices.reshape(4, 2, 2, 8, 2), ("row_0", "row_1", "col_0", "col_1", "col_2"))
    return jax.shard_map(
        local,
        mesh=finer,
        in_specs=(
            P(ROW, COL),
            P(ROW, COL),
            P(ROW),
            P(COL),
            P(ROW, COL),
            P(ROW, COL),
            P(ROW),
            P(COL),
        ),
        out_specs=(P(ROW, COL), P(ROW, COL), P(ROW), P(COL), P(ROW), P(COL), P(None, COL)),
        check_vma=False,
    )
```

profile of v0, /device:TPU:1, one launch (start us, length us, event | category | flops | bytes accessed | tf_op | source)
XLA Modules:
  0.0 134.2 jit_solution(17880412056513600817)
XLA Ops:
  0.6 0.0 copy-start.2
  0.6 0.0 copy-start
  0.7 0.0 copy-start.8
  0.7 0.0 copy-start.9
  0.7 0.0 copy-start.3
  0.7 1.3 fusion.5
  2.0 1.8 %fusion.2 = (f32[768]{0:T(1024)S(1)}, f32[768]{0:T(1024)S(1)}) fusion(bf16[768,768]{1,0:T(8,128)(2,1)} %param.9), kind=kLoop, calls=%fused_computation.4 | loop fusion | flops 2947584 | bytes 1185792 | tf_op jit(solution)/shard_map/reduce_sum | solution.py:74
  3.8 0.6 broadcast_in_dim.7
  4.5 5.9 %all-to-all-start.1 = ((f32[8,1,960]{2,1,0:T(1,128)}), f32[8,1,960]{2,1,0:T(1,128)S(1)}, u32[]{:S(2)}, u32[]{:S(2)}) async-start(f32[8,1,960]{2,1,0:T(1,128)} %broadcast_in_dim.7), calls=%async_computation.1 | async-start | bytes 65536 | tf_op jit(solution)/shard_map/all_to_all | solution.py:24
  10.3 5.1 %all-to-all-done.1 = f32[8,1,960]{2,1,0:T(1,128)S(1)} async-done(((f32[8,1,960]{2,1,0:T(1,128)}), f32[8,1,960]{2,1,0:T(1,128)S(1)}, u32[]{:S(2)}, u32[]{:S(2)}) %all-to-all-start.1) | async-done | bytes 30752 | tf_op jit(solution)/shard_map/all_to_all | solution.py:24
  15.4 0.8 broadcast_in_dim.6
  16.2 13.0 %all-to-all-start = ((f32[32,1,1536]{2,1,0:T(1,128)}), f32[32,1,1536]{2,1,0:T(1,128)S(1)}, u32[]{:S(2)}, u32[]{:S(2)}) async-start(f32[32,1,1536]{2,1,0:T(1,128)} %broadcast_in_dim.6), calls=%async_computation | async-start | bytes 393216 | tf_op jit(solution)/shard_map/all_to_all | solution.py:24
  29.3 0.7 multiply_add_fusion.1
  29.9 0.0 copy-start.7
  29.9 0.7 multiply_add_fusion
  30.6 0.0 copy-start.5
  30.6 10.2 %all-to-all-done = f32[32,1,1536]{2,1,0:T(1,128)S(1)} async-done(((f32[32,1,1536]{2,1,0:T(1,128)}), f32[32,1,1536]{2,1,0:T(1,128)S(1)}, u32[]{:S(2)}, u32[]{:S(2)}) %all-to-all-start) | async-done | bytes 196640 | tf_op jit(solution)/shard_map/all_to_all | solution.py:24
  40.8 0.1 reduce_sum.93
  41.0 0.0 copy-done.8
  41.0 0.0 copy-done.9
  41.0 0.0 copy-start.4
  41.0 0.0 copy-start.6
  41.0 0.0 copy-done.2
  41.0 0.0 copy-done.3
  41.0 0.9 multiply_reduce_fusion.2
  41.9 0.0 copy-done
  41.9 3.3 %multiply_reduce_fusion = (f32[]{:T(128)}, f32[]{:T(128)}) fusion(bf16[768,768]{1,0:T(8,128)(2,1)S(1)} %copy-done, f32[768]{0:T(1024)S(1)} %multiply_add_fusion, f32[768]{0:T(1024)S(1)} %get-tuple-element.34, f32[768,768]{1,0:T(8,128)} %param.8), kind=kLoop, calls=%fused_computation.6 | loop fusion | flops 4128766 | bytes 3545096 | tf_op jit(solution)/shard_map/reduce_sum | solution.py:87
  45.2 7.6 %all-reduce.1 = (f32[]{:T(128)}, f32[]{:T(128)}, f32[]{:T(128)}, f32[]{:T(128)}) all-reduce(f32[]{:T(128)} %get-tuple-element.35, f32[]{:T(128)} %get-tuple-element.36, f32[]{:T(128)} %get-tuple-element.37, f32[]{:T(128)} %get-tuple-element.38), channel_id=1, replica_groups=mesh['row_0'=4,'row_1'=2,'col_0'=2,'col_1'=8,'col_2'=2] {'row_0'}, use_global_device_ids=true, to_apply=%region_13.0 | all-reduce | flops 4 | bytes 32 | tf_op jit(solution)/shard_map/psum | solution.py:18
  52.8 4.4 %all-reduce.4 = (f32[]{:T(128)}, f32[]{:T(128)}, f32[]{:T(128)}, f32[]{:T(128)}) all-reduce(f32[]{:T(128)} %get-tuple-element.15, f32[]{:T(128)} %get-tuple-element.16, f32[]{:T(128)} %get-tuple-element.17, f32[]{:T(128)} %get-tuple-element.18), channel_id=1, replica_groups=mesh['row_0'=4,'row_1'=2,'col_0'=2,'col_1'=8,'col_2'=2] {'row_1'}, use_global_device_ids=true, to_apply=%region_14.0 | all-reduce | flops 4 | bytes 32 | tf_op jit(solution)/shard_map/psum | solution.py:18
  57.2 5.9 %all-reduce.3 = (f32[]{:T(128)}, f32[]{:T(128)}, f32[]{:T(128)}, f32[]{:T(128)}) all-reduce(f32[]{:T(128)} %get-tuple-element.27, f32[]{:T(128)} %get-tuple-element.28, f32[]{:T(128)} %get-tuple-element.29, f32[]{:T(128)} %get-tuple-element.30), channel_id=1, replica_groups=mesh['row_0'=4,'row_1'=2,'col_0'=2,'col_1'=8,'col_2'=2] {'col_0'}, use_global_device_ids=true, to_apply=%region_15.0 | all-reduce | flops 4 | bytes 32 | tf_op jit(solution)/shard_map/psum | solution.py:18
  63.2 12.3 %all-reduce = (f32[]{:T(128)}, f32[]{:T(128)}, f32[]{:T(128)}, f32[]{:T(128)}) all-reduce(f32[]{:T(128)} %get-tuple-element.23, f32[]{:T(128)} %get-tuple-element.24, f32[]{:T(128)} %get-tuple-element.25, f32[]{:T(128)} %get-tuple-element.26), channel_id=1, replica_groups=mesh['row_0'=4,'row_1'=2,'col_0'=2,'col_1'=8,'col_2'=2] {'col_1'}, use_global_device_ids=true, to_apply=%region_16.0 | all-reduce | flops 4 | bytes 32 | tf_op jit(solution)/shard_map/psum | solution.py:18
  75.5 12.2 %all-reduce.2 = (f32[]{:T(128)}, f32[]{:T(128)}, f32[]{:T(128)}, f32[]{:T(128)}) all-reduce(f32[]{:T(128)} %get-tuple-element.11, f32[]{:T(128)} %get-tuple-element.12, f32[]{:T(128)} %get-tuple-element.13, f32[]{:T(128)} %get-tuple-element.14), channel_id=1, replica_groups=mesh['row_0'=4,'row_1'=2,'col_0'=2,'col_1'=8,'col_2'=2] {'col_2'}, use_global_device_ids=true, to_apply=%region_17.0 | all-reduce | flops 4 | bytes 32 | tf_op jit(solution)/shard_map/psum | solution.py:18
  89.0 0.0 copy-done.7
  89.0 1.0 fusion.8
  90.0 0.0 copy-done.4
  90.0 1.6 %broadcast_in_dim.8 = bf16[8,768,192]{1,2,0:T(8,128)(2,1)} broadcast(bf16[768,192]{0,1:T(8,128)(2,1)S(1)} %get-tuple-element.31), dimensions={1,2} | broadcast | bytes 2654208 | tf_op jit(solution)/shard_map/broadcast_in_dim | solution.py:25
  91.6 0.0 copy-start.1
  91.6 4.5 %all-to-all-start.2 = ((bf16[8,768,192]{1,2,0:T(8,128)(2,1)}), bf16[8,768,192]{1,2,0:T(8,128)(2,1)}, u32[]{:S(2)}, u32[]{:S(2)}) async-start(bf16[8,768,192]{1,2,0:T(8,128)(2,1)} %broadcast_in_dim.8), calls=%async_computation.2 | async-start | bytes 4718592 | tf_op jit(solution)/shard_map/all_to_all | solution.py:24
  97.4 0.0 copy-done.5
  97.4 0.0 copy-done.6
  97.4 0.0 copy-done.1
  97.4 2.0 %multiply_subtract_fusion = f32[768,768]{1,0:T(8,128)} fusion(f32[768,768]{1,0:T(8,128)S(1)} %copy-done.1, bf16[768,768]{1,0:T(8,128)(2,1)S(1)} %copy-done, f32[]{:T(128)S(6)} %max.6, f32[768]{0:T(1024)S(1)} %multiply_add_fusion, f32[768]{0:T(1024)S(1)} %get-tuple-element.34, f32[]{:T(128)S(6)} %mul.78), kind=kLoop, calls=%fused_computation.5 | loop fusion | flops 3538944 | bytes 5904392 | tf_op jit(solution)/shard_map/sub | solution.py:93
  99.4 31.4 %all-to-all-done.2 = bf16[8,768,192]{1,2,0:T(8,128)(2,1)} async-done(((bf16[8,768,192]{1,2,0:T(8,128)(2,1)}), bf16[8,768,192]{1,2,0:T(8,128)(2,1)}, u32[]{:S(2)}, u32[]{:S(2)}) %all-to-all-start.2) | async-done | bytes 2359328 | tf_op jit(solution)/shard_map/all_to_all | solution.py:24
  130.8 3.3 %copy.26 = bf16[8,24,8,768]{3,2,0,1:T(8,128)(2,1)} copy(bf16[8,24,8,768]{3,2,1,0:T(8,128)(2,1)} %bitcast) | data formatting | bytes 4718592 | tf_op jit(solution)/shard_map/reshape | solution.py:44
  (4 shorter events, 0.1 us)
Async XLA Ops:
  0.6 40.4 %copy-start.2 = (bf16[768,192]{0,1:T(8,128)(2,1)S(1)}, bf16[768,192]{0,1:T(8,128)(2,1)}, u32[]{:S(2)}) copy-start(bf16[768,192]{0,1:T(8,128)(2,1)} %param.13) | copy-start | bytes 884740
  0.6 41.3 %copy-start = (bf16[768,768]{1,0:T(8,128)(2,1)S(1)}, bf16[768,768]{1,0:T(8,128)(2,1)}, u32[]{:S(2)}) copy-start(bf16[768,768]{1,0:T(8,128)(2,1)} %param.9) | copy-start | bytes 3538948
  0.7 40.3 %copy-start.8 = (f32[768]{0:T(1024)S(1)}, f32[768]{0:T(1024)}, u32[]{:S(2)}) copy-start(f32[768]{0:T(1024)} %param.14) | copy-start | bytes 9220
  0.7 40.3 %copy-start.9 = (f32[768]{0:T(1024)S(1)}, f32[768]{0:T(1024)}, u32[]{:S(2)}) copy-start(f32[768]{0:T(1024)} %param.10) | copy-start | bytes 9220
  0.7 40.4 %copy-start.3 = (f32[768,192]{0,1:T(8,128)S(1)}, f32[768,192]{0,1:T(8,128)}, u32[]{:S(2)}) copy-start(f32[768,192]{0,1:T(8,128)} %param.12) | copy-start | bytes 1769476
  4.5 11.0 %all-to-all-start.1 = ((f32[8,1,960]{2,1,0:T(1,128)}), f32[8,1,960]{2,1,0:T(1,128)S(1)}, u32[]{:S(2)}, u32[]{:S(2)}) async-start(f32[8,1,960]{2,1,0:T(1,128)} %broadcast_in_dim.7), calls=%async_computation.1 | async-start | bytes 65536 | tf_op jit(solution)/shard_map/all_to_all | solution.py:24
  16.2 24.6 %all-to-all-start = ((f32[32,1,1536]{2,1,0:T(1,128)}), f32[32,1,1536]{2,1,0:T(1,128)S(1)}, u32[]{:S(2)}, u32[]{:S(2)}) async-start(f32[32,1,1536]{2,1,0:T(1,128)} %broadcast_in_dim.6), calls=%async_computation | async-start | bytes 393216 | tf_op jit(solution)/shard_map/all_to_all | solution.py:24
  29.9 59.1 %copy-start.7 = (f32[192]{0:T(256)}, f32[192]{0:T(256)S(1)}, u32[]{:S(2)}) copy-start(f32[192]{0:T(256)S(1)} %multiply_add_fusion.1) | copy-start | bytes 2308
  30.6 66.8 %copy-start.5 = (f32[768]{0:T(1024)}, f32[768]{0:T(1024)S(1)}, u32[]{:S(2)}) copy-start(f32[768]{0:T(1024)S(1)} %multiply_add_fusion) | copy-start | bytes 9220
  41.0 49.1 %copy-start.4 = (f32[768]{0:T(1024)}, f32[768]{0:T(1024)S(1)}, u32[]{:S(2)}) copy-start(f32[768]{0:T(1024)S(1)} %get-tuple-element.33) | copy-start | bytes 9220
  41.0 56.4 %copy-start.6 = (f32[768]{0:T(1024)}, f32[768]{0:T(1024)S(1)}, u32[]{:S(2)}) copy-start(f32[768]{0:T(1024)S(1)} %get-tuple-element.34) | copy-start | bytes 9220
  91.6 5.8 %copy-start.1 = (f32[768,768]{1,0:T(8,128)S(1)}, f32[768,768]{1,0:T(8,128)}, u32[]{:S(2)}) copy-start(f32[768,768]{1,0:T(8,128)} %param.8) | copy-start | bytes 7077892
  91.6 39.2 %all-to-all-start.2 = ((bf16[8,768,192]{1,2,0:T(8,128)(2,1)}), bf16[8,768,192]{1,2,0:T(8,128)(2,1)}, u32[]{:S(2)}, u32[]{:S(2)}) async-start(bf16[8,768,192]{1,2,0:T(8,128)(2,1)} %broadcast_in_dim.8), calls=%async_computation.2 | async-start | bytes 4718592 | tf_op jit(solution)/shard_map/all_to_all | solution.py:24
where the time goes:
time: 135 us; the launch traced here: 134 us
  waiting for transfers between devices  46.7 us (35%)
  blocking collectives  42.5 us (31%)
  starting transfers between devices  23.4 us (17%)
  other arithmetic  11.9 us (9%)
  local copies, waits for them, and re-layouts  6.37 us (5%)
  between operations  3.36 us (2%)
    all_to_all x3, waiting for transfers between devices, from_everyone(): lax.all_to_all(jnp.broadcast_to(value[None], (length, *value.shape)), axi...  46.7 us
    psum x5, blocking collectives, over_axes(): value = lax.psum(value, axis)  42.5 us
    all_to_all x3, starting transfers between devices, from_everyone(): lax.all_to_all(jnp.broadcast_to(value[None], (length, *value.shape)), axi...  23.4 us
    reduce_sum x2, other arithmetic, local(): clip_local = (jnp.sum(jnp.square(mlp_raw)), jnp.sum(jnp.square(attn_raw)))  4.2 us
    reshape x1, local copies, waits for them, and re-layouts, in_order(): pieces.reshape(*dims[:dim], dims[dim] * dims[dim + 1], *dims[dim + 2:])  3.35 us
    broadcast_in_dim x3, local copies, waits for them, and re-layouts, from_everyone(): jnp.broadcast_to(value[None], (length, *value.shape))  2.97 us
  transfers between devices with their start and end apart: 3, of which 3 were waited for; matrix products, arithmetic and copies ran while one was open for 3% of the time, Pallas kernels for 0%

commit v1 on v0

--- a/solution.py
+++ b/solution.py
@@ -15,7 +15,8 @@
 
 def over_axes(value, axes):
     for axis in axes:
-        value = lax.psum(value, axis)
+        low = lax.all_gather(value, axis)
+        value = jnp.sum(low, axis=0)
     return value
 
 

time: 135 us -> 173 us (1.28)
  local copies, waits for them, and re-layouts: 6.37 us -> 37.4 us
  other arithmetic: 11.9 us -> 26.9 us
  waiting for transfers between devices: 46.7 us -> 40.4 us
    psum x5 -> x0, blocking collectives: 42.5 us -> none  [over_axes(): value = lax.psum(value, axis)]
    unnamed x0 -> x5, blocking collectives: none -> 41.6 us
    unnamed x20 -> x79, local copies, waits for them, and re-layouts: 0.05 us -> 31.1 us
    reduce_sum x0 -> x22, other arithmetic: none -> 18 us  [the longest x20 13.3 us: over_axes(): value = jnp.sum(low, axis=0)]
    all_to_all x3, waiting for transfers between devices: 46.7 us -> 40.4 us  [from_everyone(): lax.all_to_all(jnp.broadcast_to(value[None], (length, *value.shape)), axi...]
  transfers between devices with their start and end apart: 3 -> 3, of which waited for: 3 -> 2; matrix products, arithmetic and copies ran while one was open for 3% -> 7% of each run, Pallas kernels for 0% -> 0%
where the time goes in v1:
time: 173 us; the launch traced here: 172 us
  blocking collectives  41.6 us (24%)
  waiting for transfers between devices  40.4 us (23%)
  local copies, waits for them, and re-layouts  37.4 us (22%)
  other arithmetic  26.9 us (16%)
  starting transfers between devices  22.3 us (13%)
  between operations  3.56 us (2%)
    unnamed x5, blocking collectives  41.6 us
    all_to_all x3, waiting for transfers between devices, from_everyone(): lax.all_to_all(jnp.broadcast_to(value[None], (length, *value.shape)), axi...  40.4 us
    unnamed x79, local copies, waits for them, and re-layouts  31.1 us
    all_to_all x3, starting transfers between devices, from_everyone(): lax.all_to_all(jnp.broadcast_to(value[None], (length, *value.shape)), axi...  22.3 us
    reduce_sum x20, other arithmetic, over_axes(): value = jnp.sum(low, axis=0)  13.3 us
  transfers between devices with their start and end apart: 3, of which 2 were waited for; matrix products, arithmetic and copies ran while one was open for 7% of the time, Pallas kernels for 0%

profile of v1, /device:TPU:1, one launch (start us, length us, event | category | flops | bytes accessed | tf_op | source)
XLA Modules:
  0.0 172.1 jit_solution(3259980063333217406)
XLA Ops:
  0.6 1.2 fusion.5
  1.9 1.9 %fusion.2 = (f32[768]{0:T(1024)S(1)}, f32[768]{0:T(1024)S(1)}) fusion(bf16[768,768]{1,0:T(8,128)(2,1)} %param.9), kind=kLoop, calls=%fused_computation.4 | loop fusion | flops 2947584 | bytes 1185792 | tf_op jit(solution)/shard_map/reduce_sum | solution.py:75
  3.8 0.6 broadcast_in_dim.7
  4.4 5.9 %all-to-all-start.1 = ((f32[8,1,960]{2,1,0:T(1,128)}), f32[8,1,960]{2,1,0:T(1,128)S(1)}, u32[]{:S(2)}, u32[]{:S(2)}) async-start(f32[8,1,960]{2,1,0:T(1,128)} %broadcast_in_dim.7), calls=%async_computation.1 | async-start | bytes 65536 | tf_op jit(solution)/shard_map/all_to_all | solution.py:25
  10.3 1.8 %multiply_reduce_fusion.3 = f32[]{:T(128)} fusion(f32[768,192]{0,1:T(8,128)} %param.12), kind=kLoop, calls=%fused_computation.15 | loop fusion | flops 294911 | bytes 589828 | tf_op jit(solution)/shard_map/reduce_sum | solution.py:72
  12.1 3.0 %multiply_reduce_fusion.1 = f32[]{:T(128)} fusion(f32[768,768]{1,0:T(8,128)} %param.8), kind=kLoop, calls=%fused_computation.7 | loop fusion | flops 1179647 | bytes 2359300 | tf_op jit(solution)/shard_map/reduce_sum | solution.py:72
  15.1 0.6 dynamic-slice
  15.7 1.4 dynamic-update-slice
  17.1 1.4 dynamic-update-slice.10
  18.5 0.8 broadcast_in_dim.6
  19.3 11.9 %all-to-all-start = ((f32[32,1,1536]{2,1,0:T(1,128)}), f32[32,1,1536]{2,1,0:T(1,128)S(1)}, u32[]{:S(2)}, u32[]{:S(2)}) async-start(f32[32,1,1536]{2,1,0:T(1,128)} %broadcast_in_dim.6), calls=%async_computation | async-start | bytes 393216 | tf_op jit(solution)/shard_map/all_to_all | solution.py:25
  31.3 11.5 %all-to-all-done = f32[32,1,1536]{2,1,0:T(1,128)S(1)} async-done(((f32[32,1,1536]{2,1,0:T(1,128)}), f32[32,1,1536]{2,1,0:T(1,128)S(1)}, u32[]{:S(2)}, u32[]{:S(2)}) %all-to-all-start) | async-done | bytes 196640 | tf_op jit(solution)/shard_map/all_to_all | solution.py:25
  43.0 1.6 multiply_reduce_fusion
  44.6 1.4 dynamic-update-slice.5
  46.0 0.9 multiply_reduce_fusion.2
  46.9 1.4 dynamic-update-slice.15
  48.3 0.6 dynamic-slice.1
  48.9 8.9 %all-reduce.21 = (f32[4]{0:T(128)S(1)}, f32[4]{0:T(128)S(1)}, f32[4]{0:T(128)S(1)}, f32[4]{0:T(128)S(1)}) all-reduce(f32[4]{0:T(128)S(1)} %dynamic-update-slice.5, f32[4]{0:T(128)S(1)} %dynamic-update-slice, f32[4]{0:T(128)S(1)} %dynamic-update-slice.15, ...), channel_id=1, replica_groups=mesh['row_0'=4,'row_1'=2,'col_0'=2,'col_1'=8,'col_2'=2] {'row_0'}, use_global_device_ids=true, to_apply=%add.5 | all-reduce | flops 16 | bytes 128
  57.8 0.6 reduce_sum.289
  58.4 0.6 reduce_sum.295
  59.0 1.4 dynamic-update-slice.11
  60.4 1.4 dynamic-update-slice.16
  61.8 0.6 reduce_sum.271
  62.4 0.6 reduce_sum.283
  63.0 1.4 dynamic-update-slice.6
  64.4 1.4 dynamic-update-slice.1
  66.4 3.8 %all-reduce.24 = (f32[2]{0:T(128)S(1)}, f32[2]{0:T(128)S(1)}, f32[2]{0:T(128)S(1)}, f32[2]{0:T(128)S(1)}) all-reduce(f32[2]{0:T(128)S(1)} %dynamic-update-slice.6, f32[2]{0:T(128)S(1)} %dynamic-update-slice.1, f32[2]{0:T(128)S(1)} %dynamic-update-slice.16, ...), channel_id=1, replica_groups=mesh['row_0'=4,'row_1'=2,'col_0'=2,'col_1'=8,'col_2'=2] {'row_1'}, use_global_device_ids=true, to_apply=%add.6 | all-reduce | flops 8 | bytes 64
  70.2 0.6 reduce_sum.290
  70.8 0.6 reduce_sum.296
  71.4 1.4 dynamic-update-slice.12
  72.8 1.4 dynamic-update-slice.17
  74.2 0.6 reduce_sum.272
  74.8 0.6 reduce_sum.284
  75.4 1.4 dynamic-update-slice.7
  76.8 1.4 dynamic-update-slice.2
  78.8 5.3 %all-reduce.23 = (f32[2]{0:T(128)S(1)}, f32[2]{0:T(128)S(1)}, f32[2]{0:T(128)S(1)}, f32[2]{0:T(128)S(1)}) all-reduce(f32[2]{0:T(128)S(1)} %dynamic-update-slice.7, f32[2]{0:T(128)S(1)} %dynamic-update-slice.2, f32[2]{0:T(128)S(1)} %dynamic-update-slice.17, ...), channel_id=1, replica_groups=mesh['row_0'=4,'row_1'=2,'col_0'=2,'col_1'=8,'col_2'=2] {'col_0'}, use_global_device_ids=true, to_apply=%add.7 | all-reduce | flops 8 | bytes 64
  84.0 0.6 reduce_sum.291
  84.6 0.6 reduce_sum.297
  85.2 1.4 dynamic-update-slice.13
  86.6 1.4 dynamic-update-slice.18
  88.0 0.6 reduce_sum.273
  88.6 0.6 reduce_sum.285
  89.2 1.4 dynamic-update-slice.8
  90.6 1.4 dynamic-update-slice.3
  92.6 11.6 %all-reduce.20 = (f32[8]{0:T(128)S(1)}, f32[8]{0:T(128)S(1)}, f32[8]{0:T(128)S(1)}, f32[8]{0:T(128)S(1)}) all-reduce(f32[8]{0:T(128)S(1)} %dynamic-update-slice.8, f32[8]{0:T(128)S(1)} %dynamic-update-slice.3, f32[8]{0:T(128)S(1)} %dynamic-update-slice.18, ...), channel_id=1, replica_groups=mesh['row_0'=4,'row_1'=2,'col_0'=2,'col_1'=8,'col_2'=2] {'col_1'}, use_global_device_ids=true, to_apply=%add.8 | all-reduce | flops 32 | bytes 256
  104.2 0.6 reduce_sum.292
  104.8 0.6 reduce_sum.298
  105.4 1.4 dynamic-update-slice.14
  106.8 1.4 dynamic-update-slice.19
  108.2 0.6 reduce_sum.274
  108.8 0.6 reduce_sum.286
  109.4 1.4 dynamic-update-slice.9
  110.8 1.4 dynamic-update-slice.4
  112.2 12.1 %all-reduce.22 = (f32[2]{0:T(128)}, f32[2]{0:T(128)}, f32[2]{0:T(128)S(1)}, f32[2]{0:T(128)S(1)}) all-reduce(f32[2]{0:T(128)S(1)} %dynamic-update-slice.9, f32[2]{0:T(128)S(1)} %dynamic-update-slice.4, f32[2]{0:T(128)S(1)} %dynamic-update-slice.19, ...), channel_id=1, replica_groups=mesh['row_0'=4,'row_1'=2,'col_0'=2,'col_1'=8,'col_2'=2] {'col_2'}, use_global_device_ids=true, to_apply=%add.9 | all-reduce | flops 8 | bytes 64
  124.3 0.6 reduce_sum.293
  125.6 0.6 reduce_sum.299
  126.9 1.0 fusion.8
  128.0 1.6 broadcast_in_dim.8
  129.5 4.5 %all-to-all-start.2 = ((bf16[8,768,192]{1,2,0:T(8,128)(2,1)}), bf16[8,768,192]{1,2,0:T(8,128)(2,1)}, u32[]{:S(2)}, u32[]{:S(2)}) async-start(bf16[8,768,192]{1,2,0:T(8,128)(2,1)} %broadcast_in_dim.8), calls=%async_computation.2 | async-start | bytes 4718592 | tf_op jit(solution)/shard_map/all_to_all | solution.py:25
  134.1 1.2 reduce_sum.275
  135.9 1.3 reduce_sum.287
  137.8 2.0 %multiply_subtract_fusion = f32[768,768]{1,0:T(8,128)} fusion(f32[768,768]{1,0:T(8,128)S(1)} %copy-done.1, bf16[768,768]{1,0:T(8,128)(2,1)S(1)} %copy-done, f32[]{:T(128)S(6)} %max.6, f32[768]{0:T(1024)S(1)} %multiply_add_fusion, f32[768]{0:T(1024)S(1)} %get-tuple-element.34, f32[]{:T(128)S(6)} %mul.78), kind=kLoop, calls=%fused_computation.5 | loop fusion | flops 3538944 | bytes 5904392 | tf_op jit(solution)/shard_map/sub | solution.py:94
  139.9 28.9 %all-to-all-done.2 = bf16[8,768,192]{1,2,0:T(8,128)(2,1)} async-done(((bf16[8,768,192]{1,2,0:T(8,128)(2,1)}), bf16[8,768,192]{1,2,0:T(8,128)(2,1)}, u32[]{:S(2)}, u32[]{:S(2)}) %all-to-all-start.2) | async-done | bytes 2359328 | tf_op jit(solution)/shard_map/all_to_all | solution.py:25
  168.8 3.3 %copy.26 = bf16[8,24,8,768]{3,2,0,1:T(8,128)(2,1)} copy(bf16[8,24,8,768]{3,2,1,0:T(8,128)(2,1)} %bitcast.25) | data formatting | bytes 4718592 | tf_op jit(solution)/shard_map/reshape | solution.py:45
  (65 shorter events, 2.1 us)
Async XLA Ops:
  0.6 14.5 %copy-start.16 = (u32[256]{0:T(256)S(1)}, u32[256]{0:T(256)}, u32[]{:S(2)}) copy-start(u32[256]{0:T(256)} %constant.37) | copy-start | bytes 3076
  1.8 29.4 %copy-start.11 = (f32[192]{0:T(256)S(1)}, f32[192]{0:T(256)}, u32[]{:S(2)}) copy-start(f32[192]{0:T(256)} %param.15) | copy-start | bytes 2308
  1.8 29.4 %copy-start.8 = (f32[768]{0:T(1024)S(1)}, f32[768]{0:T(1024)}, u32[]{:S(2)}) copy-start(f32[768]{0:T(1024)} %param.11) | copy-start | bytes 9220
  1.8 41.1 %copy-start.9 = (f32[768]{0:T(1024)S(1)}, f32[768]{0:T(1024)}, u32[]{:S(2)}) copy-start(f32[768]{0:T(1024)} %param.14) | copy-start | bytes 9220
  1.8 41.1 %copy-start.10 = (f32[768]{0:T(1024)S(1)}, f32[768]{0:T(1024)}, u32[]{:S(2)}) copy-start(f32[768]{0:T(1024)} %param.10) | copy-start | bytes 9220
  1.9 41.1 %copy-start = (bf16[768,768]{1,0:T(8,128)(2,1)S(1)}, bf16[768,768]{1,0:T(8,128)(2,1)}, u32[]{:S(2)}) copy-start(bf16[768,768]{1,0:T(8,128)(2,1)} %param.9) | copy-start | bytes 3538948
  4.4 14.1 %all-to-all-start.1 = ((f32[8,1,960]{2,1,0:T(1,128)}), f32[8,1,960]{2,1,0:T(1,128)S(1)}, u32[]{:S(2)}, u32[]{:S(2)}) async-start(f32[8,1,960]{2,1,0:T(1,128)} %broadcast_in_dim.7), calls=%async_computation.1 | async-start | bytes 65536 | tf_op jit(solution)/shard_map/all_to_all | solution.py:25
  12.1 33.9 %copy-start.2 = (bf16[768,192]{0,1:T(8,128)(2,1)S(1)}, bf16[768,192]{0,1:T(8,128)(2,1)}, u32[]{:S(2)}) copy-start(bf16[768,192]{0,1:T(8,128)(2,1)} %param.13) | copy-start | bytes 884740
  12.1 36.2 %copy-start.15 = (u32[256]{0:T(256)S(1)}, u32[256]{0:T(256)}, u32[]{:S(2)}) copy-start(u32[256]{0:T(256)} %constant.42) | copy-start | bytes 3076
  12.1 53.7 %copy-start.14 = (u32[256]{0:T(256)S(1)}, u32[256]{0:T(256)}, u32[]{:S(2)}) copy-start(u32[256]{0:T(256)} %constant.47) | copy-start | bytes 3076
  12.1 66.1 %copy-start.13 = (u32[256]{0:T(256)S(1)}, u32[256]{0:T(256)}, u32[]{:S(2)}) copy-start(u32[256]{0:T(256)} %constant.52) | copy-start | bytes 3076
  12.1 79.9 %copy-start.12 = (u32[256]{0:T(256)S(1)}, u32[256]{0:T(256)}, u32[]{:S(2)}) copy-start(u32[256]{0:T(256)} %constant.57) | copy-start | bytes 3076
  12.1 114.8 %copy-start.3 = (f32[768,192]{0,1:T(8,128)S(1)}, f32[768,192]{0,1:T(8,128)}, u32[]{:S(2)}) copy-start(f32[768,192]{0,1:T(8,128)} %param.12) | copy-start | bytes 1769476
  19.3 23.5 %all-to-all-start = ((f32[32,1,1536]{2,1,0:T(1,128)}), f32[32,1,1536]{2,1,0:T(1,128)S(1)}, u32[]{:S(2)}, u32[]{:S(2)}) async-start(f32[32,1,1536]{2,1,0:T(1,128)} %broadcast_in_dim.6), calls=%async_computation | async-start | bytes 393216 | tf_op jit(solution)/shard_map/all_to_all | solution.py:25
  31.3 98.3 %copy-start.7 = (f32[192]{0:T(256)}, f32[192]{0:T(256)S(1)}, u32[]{:S(2)}) copy-start(f32[192]{0:T(256)S(1)} %multiply_add_fusion.1) | copy-start | bytes 2308
  31.3 106.5 %copy-start.4 = (f32[768]{0:T(1024)}, f32[768]{0:T(1024)S(1)}, u32[]{:S(2)}) copy-start(f32[768]{0:T(1024)S(1)} %multiply_add_fusion) | copy-start | bytes 9220
  43.0 86.6 %copy-start.5 = (f32[768]{0:T(1024)}, f32[768]{0:T(1024)S(1)}, u32[]{:S(2)}) copy-start(f32[768]{0:T(1024)S(1)} %get-tuple-element.33) | copy-start | bytes 9220
  43.0 94.8 %copy-start.6 = (f32[768]{0:T(1024)}, f32[768]{0:T(1024)S(1)}, u32[]{:S(2)}) copy-start(f32[768]{0:T(1024)S(1)} %get-tuple-element.34) | copy-start | bytes 9220
  129.5 8.3 %copy-start.1 = (f32[768,768]{1,0:T(8,128)S(1)}, f32[768,768]{1,0:T(8,128)}, u32[]{:S(2)}) copy-start(f32[768,768]{1,0:T(8,128)} %param.8) | copy-start | bytes 7077892
  129.5 39.2 %all-to-all-start.2 = ((bf16[8,768,192]{1,2,0:T(8,128)(2,1)}), bf16[8,768,192]{1,2,0:T(8,128)(2,1)}, u32[]{:S(2)}, u32[]{:S(2)}) async-start(bf16[8,768,192]{1,2,0:T(8,128)(2,1)} %broadcast_in_dim.8), calls=%async_computation.2 | async-start | bytes 4718592 | tf_op jit(solution)/shard_map/all_to_all | solution.py:25
